TPU v7x, 8 devices: a whole 2x2x1 slice. The times are simulated.
8 devices in a mesh: dp: 1 (over z), tp: 2 (over y), ep: 4 (over x, core).
Axes of the slice: x: 2, y: 2, z: 1, core: 2. Of those that a mesh axis runs over, the one named last changes fastest.
Arguments:
- hidden: bfloat16 [256, 2048], P(('dp', 'ep'))
- expert_ids: int32 [256, 8], P(('dp', 'ep'))
- norm_w: bfloat16 [2048], replicated
- router_w: bfloat16 [2048, 64], replicated
- w_gate: bfloat16 [64, 2048, 1024], P('ep', None, 'tp')
- w_up: bfloat16 [64, 2048, 1024], P('ep', None, 'tp')
- w_down: bfloat16 [64, 1024, 2048], P('ep', 'tp')
Outputs:
- output: bfloat16 [256, 2048], P(('dp', 'ep'))
All inputs are finite; a program needn't handle non-finite values.
Results may differ from a plain program's by a relative error of at most 0.00947046.
Values are sent between devices in bfloat16 or wider.
A program may use at most 1 GiB of HBM per device.

v0:
```python
import jax
import jax.numpy as jnp
from jax import lax
from jax.sharding import PartitionSpec as P

NORM_EPS = 1e-6


def rms_norm(hidden, norm_w):
    wide_h = hidden.astype(jnp.float32)
    mean_sq = jnp.mean(wide_h * wide_h, axis=-1, keepdims=True)
    return (wide_h * lax.rsqrt(mean_sq + NORM_EPS) * norm_w.astype(jnp.float32)).astype(jnp.bfloat16)


def slot_rank(expert_ids, n_experts):
    flat_ids = expert_ids.reshape(-1)
    one_hot = (flat_ids[:, None] == jnp.arange(n_experts, dtype=jnp.int32)[None, :]).astype(jnp.int32)
    running = jnp.cumsum(one_hot, axis=0)
    return jnp.sum(running * one_hot, axis=1) - 1


def row_cap(tok_dev, top_k, n_experts):
    return 8 * ((2 * top_k * tok_dev + 8 * n_experts - 1) // (8 * n_experts))


def gather_slots(normed, slot_dest, n_slots, top_k):
    pair_tok = jnp.arange(slot_dest.shape[0], dtype=jnp.int32) // top_k
    src_tok = jnp.zeros((n_slots,), jnp.int32).at[slot_dest].set(pair_tok)
    filled = jnp.zeros((n_slots,), jnp.int32).at[slot_dest].set(1)
    return jnp.where(filled[:, None] > 0, normed[src_tok], jnp.zeros((), jnp.bfloat16))


def solution(mesh):
    ep_size = mesh.shape["ep"]

    def per_device(hidden, expert_ids, norm_w, router_w, w_gate, w_up, w_down):
        tok_dev, model_dim = hidden.shape
        top_k = expert_ids.shape[1]
        n_experts = router_w.shape[1]
        local_exp = w_gate.shape[0]
        row_limit = row_cap(tok_dev, top_k, n_experts)
        n_slots = n_experts * row_limit
        normed = rms_norm(hidden, norm_w)
        logits = jnp.dot(normed, router_w, preferred_element_type=jnp.float32)
        gate_prob = jnp.take_along_axis(jax.nn.softmax(logits, axis=-1), expert_ids, axis=-1)
        slot_dest = expert_ids.reshape(-1) * row_limit + slot_rank(expert_ids, n_experts)
        send_rows = gather_slots(normed, slot_dest, n_slots, top_k).reshape(ep_size, local_exp, row_limit, model_dim)
        recv_rows = lax.all_to_all(send_rows, "ep", 0, 2, tiled=True).reshape(local_exp, ep_size * row_limit, model_dim)
        gate_pre = jnp.einsum("erd,edf->erf", recv_rows, w_gate, preferred_element_type=jnp.float32)
        up_pre = jnp.einsum("erd,edf->erf", recv_rows, w_up, preferred_element_type=jnp.float32)
        act_rows = (jax.nn.silu(gate_pre) * up_pre).astype(jnp.bfloat16)
        part_out = jnp.einsum("erf,efd->erd", act_rows, w_down, preferred_element_type=jnp.float32).astype(jnp.bfloat16)
        expert_out = lax.psum(part_out, "tp")
        back_rows = lax.all_to_all(expert_out.reshape(1, local_exp, ep_size * row_limit, model_dim), "ep", 2, 0, tiled=True)
        picked = back_rows.reshape(n_slots, model_dim)[slot_dest].reshape(tok_dev, top_k, model_dim)
        moe_sum = jnp.sum(picked.astype(jnp.float32) * gate_prob[:, :, None], axis=1)
        return (hidden.astype(jnp.float32) + moe_sum).astype(jnp.bfloat16)

    token_spec = P(("dp", "ep"), None)
    return jax.shard_map(per_device, mesh=mesh, in_specs=(token_spec, token_spec, P(None), P(None, None), P("ep", None, "tp"), P("ep", None, "tp"), P("ep", "tp", None)), out_specs=token_spec, check_vma=False)
```

profile of v0, /device:TPU:0, one launch (start us, length us, event | category | flops | bytes accessed | tf_op | source)
XLA Modules:
  0.0 309.1 jit_solution(1101508525515118304)
XLA Ops:
  6.5 0.0 copy-start
  6.5 0.0 all-reduce.2.cloned.1.call-start
  6.5 0.7 broadcast_multiply_fusion
  7.3 0.8 copy.36
  8.0 0.1 eq.29
  8.1 0.1 eq.25
  8.2 1.1 fusion.1
  9.3 0.7 convert_element_type.32
  10.0 0.1 copy.35
  10.1 0.1 mul.55
  10.2 1.2 reduce-window.6
  11.4 0.2 slice_reduce_fusion
  11.7 0.1 fusion.6
  11.9 2.4 scatter_custom_fusion.1
  14.3 2.4 scatter_custom_fusion
  16.8 0.1 broadcast_in_dim.20
  16.9 1.1 fusion.3
  18.0 6.0 %gather_fusion = bf16[1024,2048]{1,0:T(8,128)(2,1)} fusion(bf16[64,2048]{1,0:T(8,128)(2,1)S(1)} %fusion.3, s32[1024]{0:T(1024)S(1)} %fusion.10), kind=kCustom, calls=%fused_computation | custom fusion | bytes 8392704 | tf_op jit(solution)/shard_map/gather | solution.py:30
  24.0 2.5 broadcast_select_fusion
  26.6 52.5 %all_to_all.30 = bf16[4,16,16,2048]{3,2,1,0:T(8,128)(2,1)S(1)} all-to-all(bf16[4,16,16,2048]{3,2,1,0:T(8,128)(2,1)S(1)} %broadcast_select_fusion), channel_id=1, replica_groups=mesh['dp'=1,'tp'=2,'ep'=4] {'ep'}, dimensions={0} | all-to-all | bytes 8388608 | tf_op jit(solution)/shard_map/all_to_all | solution.py:48
  79.1 2.4 copy.39
  81.5 14.6 %fusion.20 = f32[16,64,512]{2,1,0:T(8,128)S(1)} fusion(bf16[16,64,2048]{2,1,0:T(8,128)(2,1)} %bitcast.45, bf16[16,2048,512]{2,1,0:T(8,128)(2,1)} %param.11), kind=kOutput, calls=%fused_computation.52 | convolution fusion | flops 2147483648 | bytes 39845888 | tf_op jit(solution)/shard_map/erd,edf->erf/dot_general | solution.py:49
  96.1 28.2 %convert_bitcast_fusion = bf16[1,16,64,2048]{3,2,1,0:T(8,128)(2,1)} fusion(bf16[16,512,2048]{2,1,0:T(8,128)(2,1)} %param.13, f32[16,64,512]{2,1,0:T(8,128)S(1)} %fusion.20, bf16[16,64,2048]{2,1,0:T(8,128)(2,1)} %bitcast.46, bf16[16,2048,512]{2,1,0:T(8,128)(2,1)} %param.12), kind=kOutput, calls=%fused_computation.7 | convolution fusion | flops 4300210176 | bytes 77594624 | tf_op jit(solution)/shard_map/erf,efd->erd/dot_general | solution.py:52
  124.3 0.0 all-reduce.2.cloned.1.call-update
  124.3 102.3 %all-reduce.2.cloned.1.call-done = bf16[1,16,64,2048]{3,2,1,0:T(8,128)(2,1)} async-done(((bf16[1,16,64,2048]{3,2,1,0:T(8,128)(2,1)}), bf16[1,16,64,2048]{3,2,1,0:T(8,128)(2,1)}) %all-reduce.2.cloned.1.call-update) | async-done | bytes 4194320 | tf_op jit(solution)/shard_map/psum | solution.py:53
  226.6 6.5 %copy.40 = bf16[1,16,64,2048]{3,1,0,2:T(8,128)(2,1)} copy(bf16[1,16,64,2048]{3,2,1,0:T(8,128)(2,1)} %all-reduce.2.cloned.1.call-done) | data formatting | bytes 8388608 | tf_op jit(solution)/shard_map/psum | solution.py:53
  233.0 0.0 copy-start.2
  233.0 5.2 %all-to-all-start.1 = ((bf16[1,16,64,2048]{3,1,0,2:T(8,128)(2,1)}), bf16[1,16,64,2048]{3,1,0,2:T(8,128)(2,1)}, u32[]{:S(2)}, u32[]{:S(2)}) async-start(bf16[1,16,64,2048]{3,1,0,2:T(8,128)(2,1)} %copy.40), calls=%async_computation.1 | async-start | bytes 8388608 | tf_op jit(solution)/shard_map/all_to_all | solution.py:54
  238.2 0.0 copy-done.2
  238.2 0.1 copy.42
  238.3 0.1 reshape.118
  238.4 0.0 copy-done
  238.4 0.2 fusion.19
  238.7 3.9 %gather_fusion.2 = f32[512]{0:T(512)S(1)} fusion(f32[64,64]{0,1:T(8,128)S(1)} %fusion.8, s32[512]{0:T(512)S(1)} %reshape.118), kind=kCustom, calls=%fused_computation.2 | custom fusion | bytes 8192 | tf_op jit(solution)/shard_map/jit(take_along_axis)/gather | solution.py:45
  242.6 0.1 reshape.121
  242.7 0.1 copy.43
  242.8 0.1 copy.44
  242.9 43.0 %all-to-all-done.1 = bf16[1,16,64,2048]{3,1,0,2:T(8,128)(2,1)} async-done(((bf16[1,16,64,2048]{3,1,0,2:T(8,128)(2,1)}), bf16[1,16,64,2048]{3,1,0,2:T(8,128)(2,1)}, u32[]{:S(2)}, u32[]{:S(2)}) %all-to-all-start.1) | async-done | bytes 4194336 | tf_op jit(solution)/shard_map/all_to_all | solution.py:54
  285.9 6.5 %copy.41 = bf16[1,16,4,16,2048]{4,3,1,2,0:T(8,128)(2,1)} copy(bf16[1,16,4,16,2048]{4,1,3,2,0:T(8,128)(2,1)} %bitcast.8) | data formatting | bytes 8388608 | tf_op jit(solution)/shard_map/all_to_all | solution.py:54
  292.4 0.0 copy-start.1
  292.4 7.2 %gather_fusion.1 = bf16[512,2048]{1,0:T(8,128)(2,1)S(1)} fusion(bf16[1024,2048]{1,0:T(8,128)(2,1)} %bitcast.44, s32[1024]{0:T(1024)S(1)} %pad_clamp_fusion), kind=kCustom, calls=%fused_computation.1 | custom fusion | bytes 4196352 | tf_op jit(solution)/shard_map/gather | solution.py:55
  299.6 1.8 fusion
  301.4 0.0 copy-done.1
  301.4 0.8 fusion.4
  (15 shorter events, 0.2 us)
Async XLA Ops:
  6.5 231.9 %copy-start = (bf16[2048,64]{0,1:T(8,128)(2,1)S(1)}, bf16[2048,64]{0,1:T(8,128)(2,1)}, u32[]{:S(2)}) copy-start(bf16[2048,64]{0,1:T(8,128)(2,1)} %param.10) | copy-start | bytes 786436
  6.5 220.0 %all-reduce.2.cloned.1.call-start = ((), (), s32[]{:S(2)}) async-start(), calls=%async_computation.2 | async-start | bytes 8388608 | tf_op jit(solution)/shard_map/psum | solution.py:53
  233.0 5.2 %copy-start.2 = (s32[64,8]{0,1:T(8,128)S(1)}, s32[64,8]{0,1:T(8,128)}, u32[]{:S(2)}) copy-start(s32[64,8]{0,1:T(8,128)} %param.8) | copy-start | bytes 6148
  233.0 52.9 %all-to-all-start.1 = ((bf16[1,16,64,2048]{3,1,0,2:T(8,128)(2,1)}), bf16[1,16,64,2048]{3,1,0,2:T(8,128)(2,1)}, u32[]{:S(2)}, u32[]{:S(2)}) async-start(bf16[1,16,64,2048]{3,1,0,2:T(8,128)(2,1)} %copy.40), calls=%async_computation.1 | async-start | bytes 8388608 | tf_op jit(solution)/shard_map/all_to_all | solution.py:54
  292.4 9.0 %copy-start.1 = (bf16[64,2048]{1,0:T(8,128)(2,1)S(1)}, bf16[64,2048]{1,0:T(8,128)(2,1)}, u32[]{:S(2)}) copy-start(bf16[64,2048]{1,0:T(8,128)(2,1)} %param.7) | copy-start | bytes 786436
Sparse Core Ops, SparseCore 0:
  124.4 102.0 all-reduce.1
where the time goes:
time: 310 us; the launch traced here: 309 us
  waiting for transfers between devices  145 us (47%)
  blocking collectives  52.5 us (17%)
  matrix products  43 us (14%)
  local copies, waits for them, and re-layouts  39.2 us (13%)
  between operations  13.6 us (4%)
  other arithmetic  10.3 us (3%)
  starting transfers between devices  5.17 us (2%)
    psum x1, waiting for transfers between devices, per_device(): expert_out = lax.psum(part_out, 'tp')  102 us
    all_to_all x1, blocking collectives, per_device(): lax.all_to_all(send_rows, 'ep', 0, 2, tiled=True)  52.5 us
    all_to_all x1, waiting for transfers between devices, per_device(): lax.all_to_all(expert_out.reshape(1, local_exp, ep_size * row_limit, mode...  43 us
    dot_general x1, matrix products, per_device(): jnp.einsum('erf,efd->erd', act_rows, w_down, preferred_element_type=jnp.f...  28.2 us
    dot_general x1, matrix products, per_device(): jnp.einsum('erd,edf->erf', recv_rows, w_gate, preferred_element_type=jnp....  14.6 us
    gather x1, local copies, waits for them, and re-layouts, per_device(): back_rows.reshape(n_slots, model_dim)[slot_dest]  7.18 us
    all_to_all x1, local copies, waits for them, and re-layouts, per_device(): lax.all_to_all(expert_out.reshape(1, local_exp, ep_size * row_limit, mode...  6.51 us
    psum x1, local copies, waits for them, and re-layouts, per_device(): expert_out = lax.psum(part_out, 'tp')  6.45 us
  transfers between devices with their start and end apart: 2, of which 2 were waited for; matrix products, arithmetic and copies ran while one was open for 1% of the time, Pallas kernels for 0%

commit v1 on v0

v1 whole, which is shorter than its diff:
```python
import jax
import jax.numpy as jnp
from jax import lax
from jax.experimental import pallas as pl
from jax.experimental.pallas import tpu as pltpu
from jax.sharding import PartitionSpec as P

NORM_EPS = 1e-6
LANES = 128
BLOCK = 256
PAIR_SLOTS = 10


def moe_kernel(
    hid_hbm, ids_hbm, norm_hbm, router_hbm, gate_hbm, up_hbm, down_hbm, out_hbm,
    w_buf, hid, ids, norm_buf, router, normed, prob_buf, x_buf, act, g3, y_buf,
    part, sib_in, x_out, x_in, y_out, y_in, out_buf,
    w_sem, load_sem, hid_send, hid_recv, ids_send, ids_recv,
    sib_send, sib_recv, xs_sem, xr_sem, ys_sem, yr_sem, out_sem,
):
    me = lax.axis_index("ep")
    tp = lax.axis_index("tp")
    sib = me + 1 - 2 * (me % 2)
    across = (me + 2) % 4
    twin = 1 - tp
    sib_id, across_id, twin_id = {"ep": sib}, {"ep": across}, {"tp": twin}

    tok, dim = hid.shape[1], hid.shape[2]
    n_exp = router.shape[0]
    local_exp = act.shape[0]
    inner = act.shape[2]
    top_k = ids.shape[1]
    cap = x_buf.shape[1] // 4
    n_blocks = dim // BLOCK
    f32, bf16 = jnp.float32, jnp.bfloat16

    def gate_copies(pair):
        slot = pair % PAIR_SLOTS
        return [
            pltpu.make_async_copy(gate_hbm.at[pair], w_buf.at[slot, 0], w_sem.at[slot, 0]),
            pltpu.make_async_copy(up_hbm.at[pair], w_buf.at[slot, 1], w_sem.at[slot, 1]),
        ]

    def down_copy(block, quad):
        slot = (local_exp + block) % PAIR_SLOTS
        rows = 4 * inner
        return pltpu.make_async_copy(
            down_hbm.at[pl.ds(quad * rows, rows), pl.ds(block * BLOCK, BLOCK)],
            w_buf.at[slot, quad // 2, :, pl.ds((quad % 2) * BLOCK, BLOCK)],
            w_sem.at[slot, quad],
        )

    def start_pair(pair):
        if isinstance(pair, int):
            if pair < local_exp:
                for c in gate_copies(pair):
                    c.start()
            elif pair < local_exp + n_blocks:
                for q in range(4):
                    down_copy(pair - local_exp, q).start()
            return

        @pl.when(pair < local_exp)
        def _():
            for c in gate_copies(pair):
                c.start()

        @pl.when((pair >= local_exp) & (pair < local_exp + n_blocks))
        def _():
            for q in range(4):
                down_copy(pair - local_exp, q).start()

    hid_load = pltpu.make_async_copy(hid_hbm, hid.at[0], load_sem.at[0])
    ids_load = pltpu.make_async_copy(ids_hbm, ids.at[0], load_sem.at[1])
    norm_load = pltpu.make_async_copy(norm_hbm, norm_buf, load_sem.at[2])
    router_load = pltpu.make_async_copy(router_hbm, router, load_sem.at[3])
    for c in (hid_load, ids_load, norm_load, router_load):
        c.start()
    for pair in range(PAIR_SLOTS):
        start_pair(pair)

    barrier = pltpu.get_barrier_semaphore()
    for dev in (sib_id, across_id, twin_id):
        pl.semaphore_signal(barrier, inc=1, device_id=dev, device_id_type=pl.DeviceIdType.MESH)
    pl.semaphore_wait(barrier, 3)

    def remote(src, dst, ssem, rsem, dev):
        return pltpu.make_async_remote_copy(
            src_ref=src, dst_ref=dst, send_sem=ssem, recv_sem=rsem,
            device_id=dev, device_id_type=pl.DeviceIdType.MESH,
        )

    def row_copies(j):
        src, dst, dev = ((0, 1, sib_id), (0, 2, across_id), (2, 3, sib_id))[j]
        return (
            remote(hid.at[src], hid.at[dst], hid_send.at[j], hid_recv.at[j], dev),
            remote(ids.at[src], ids.at[dst], ids_send.at[j], ids_recv.at[j], dev),
        )

    hid_load.wait()
    ids_load.wait()
    for j in (1, 0):
        for c in row_copies(j):
            c.start()
    norm_load.wait()
    router_load.wait()

    slot_iota = lax.broadcasted_iota(jnp.int32, (cap, tok), 0).astype(f32)
    exp_iota = lax.broadcasted_iota(jnp.int32, (local_exp, tok), 0) + me * local_exp
    t_row = lax.broadcasted_iota(jnp.int32, (tok, tok), 0)
    t_col = lax.broadcasted_iota(jnp.int32, (tok, tok), 1)
    before = jnp.where(t_row < t_col, 1.0, 0.0).astype(bf16)
    eye = jnp.where(t_row == t_col, 1.0, 0.0).astype(bf16)

    def prepare(k):
        acc = jnp.zeros((tok, LANES), f32)
        for i in range(dim // LANES):
            xs = hid[k, :, pl.ds(i * LANES, LANES)].astype(f32)
            acc = acc + xs * xs
        inv = lax.rsqrt(jnp.sum(acc, axis=1, keepdims=True) / dim + NORM_EPS)
        for i in range(dim // LANES):
            xs = hid[k, :, pl.ds(i * LANES, LANES)].astype(f32)
            w = norm_buf[pl.ds(i, 1), :].astype(f32)
            normed[:, pl.ds(i * LANES, LANES)] = (xs * inv * w).astype(bf16)
        logits = lax.dot_general(router[...], normed[...], (((1,), (1,)), ((), ())), preferred_element_type=f32)
        ex = jnp.exp(logits - jnp.max(logits, axis=0, keepdims=True))
        prob_buf[...] = ex / jnp.sum(ex, axis=0, keepdims=True)
        prob = prob_buf[pl.ds(pl.multiple_of(me * local_exp, local_exp), local_exp), :]
        hit = jnp.zeros((local_exp, tok), f32)
        for j in range(top_k):
            hit = hit + jnp.where(ids[k, pl.ds(j, 1), :] == exp_iota, 1.0, 0.0)
        rank = jnp.dot(hit.astype(bf16), before, preferred_element_type=f32)
        rank = jnp.where(hit > 0.5, rank, -1.0)
        place, weight = [], []
        for e in range(local_exp):
            here = rank[e : e + 1, :] == slot_iota
            place.append(jnp.where(here, 1.0, 0.0))
            weight.append(jnp.where(here, prob[e : e + 1, :], 0.0))
        place = jnp.concatenate(place, axis=0).astype(bf16)
        weight = jnp.concatenate(weight, axis=0)
        for p in range(3):
            piece = weight.astype(bf16)
            if p < 2:
                weight = weight - piece.astype(f32)
            g3[k, pl.ds(p * tok, tok), :] = lax.dot_general(
                eye, piece, (((1,), (1,)), ((), ())), preferred_element_type=f32
            ).astype(bf16)
        for c in range(dim // 512):
            rows = jnp.dot(place, normed[:, pl.ds(c * 512, 512)], preferred_element_type=f32).astype(bf16)
            x_buf[:, pl.ds(k * cap, cap), pl.ds(c * 512, 512)] = rows.reshape(local_exp, cap, 512)

    prepare(0)
    for c in row_copies(0):
        c.wait_recv()
    prepare(1)
    for c in row_copies(1):
        c.wait_recv()
    for c in row_copies(2):
        c.start()
    prepare(2)
    for c in row_copies(2):
        c.wait_recv()
    prepare(3)

    def expert_step(e, carry):
        slot = e % PAIR_SLOTS
        gate_copy, up_copy = gate_copies(e)
        gate_copy.wait()
        gate_pre = jnp.dot(x_buf[e], w_buf[slot, 0], preferred_element_type=f32)
        up_copy.wait()
        up_pre = jnp.dot(x_buf[e], w_buf[slot, 1], preferred_element_type=f32)
        act[e] = (jax.nn.silu(gate_pre) * up_pre).astype(bf16)

        start_pair(e + PAIR_SLOTS)
        return carry

    lax.fori_loop(0, local_exp, expert_step, 0)

    def sib_copies(b):
        return [
            remote(part.at[b, src], sib_in.at[b, i], sib_send.at[b, i], sib_recv.at[b, i], sib_id)
            for i, src in ((1, 3), (0, 1))
        ]

    def x_copy(b):
        return remote(x_out.at[b], x_in.at[b], xs_sem.at[b], xr_sem.at[b], across_id)

    def y_copy(b):
        return remote(y_out.at[b], y_in.at[b], ys_sem.at[b], yr_sem.at[b], twin_id)

    def out_copy(b):
        cols = pl.ds(b * BLOCK, BLOCK)
        return pltpu.make_async_copy(out_buf.at[:, cols], out_hbm.at[:, cols], out_sem.at[b])

    def down_quad(b, q):
        slot = (local_exp + b) % PAIR_SLOTS
        down_copy(b, q).wait()
        for i in range(4):
            e = 4 * q + i
            w = w_buf[slot, q // 2, pl.ds(i * inner, inner), pl.ds((q % 2) * BLOCK, BLOCK)]
            y = jnp.dot(act[e], w, preferred_element_type=f32).astype(bf16)
            for k in range(4):
                y_buf[k, pl.ds(e * cap, cap), :] = y[k * cap : (k + 1) * cap, :]

    def combine(b):
        for k in (3, 1, 2, 0):
            s = jnp.dot(g3[k], y_buf[k], preferred_element_type=f32)
            part[b, k] = s[:tok] + s[tok : 2 * tok] + s[2 * tok :]
            if k == 1:
                for c in sib_copies(b):
                    c.start()

    def stage_x(b):
        first, second = sib_copies(b)
        first.wait_recv()
        x_out[b] = part[b, 2] + sib_in[b, 1]
        x_copy(b).start()
        second.wait_recv()
        y_out[b] = part[b, 0] + sib_in[b, 0]

    def stage_y(b):
        x_copy(b).wait_recv()
        y_out[b] = y_out[b] + x_in[b]
        y_copy(b).start()

    def finish(b):
        y_copy(b).wait_recv()
        cols = pl.ds(b * BLOCK, BLOCK)
        out_buf[:, cols] = (hid[0, :, cols].astype(f32) + (y_out[b] + y_in[b])).astype(bf16)
        out_copy(b).start()

    Y_LAG, OUT_LAG = 4, 7
    for b in range(n_blocks):
        for q in range(4):
            down_quad(b, q)
            if q == 2 and b >= 1:
                stage_x(b - 1)
        combine(b)
        start_pair(local_exp + b + PAIR_SLOTS)
        if b >= Y_LAG:
            stage_y(b - Y_LAG)
        if b >= OUT_LAG:
            finish(b - OUT_LAG)
    stage_x(n_blocks - 1)
    for b in range(n_blocks - Y_LAG, n_blocks):
        stage_y(b)
    for b in range(n_blocks - OUT_LAG, n_blocks):
        finish(b)

    for j in range(3):
        for c in row_copies(j):
            c.wait_send()
    for b in range(n_blocks):
        for c in sib_copies(b):
            c.wait_send()
        x_copy(b).wait_send()
        y_copy(b).wait_send()
        out_copy(b).wait()


def solution(mesh):
    def per_device(hidden, expert_ids, norm_w, router_w, w_gate, w_up, w_down):
        tok, dim = hidden.shape
        top_k = expert_ids.shape[1]
        n_exp = router_w.shape[1]
        local_exp, _, inner = w_gate.shape
        cap = 8 * ((2 * top_k * tok + 8 * n_exp - 1) // (8 * n_exp))
        nb = dim // BLOCK
        f32, bf16 = jnp.float32, jnp.bfloat16
        dma = pltpu.SemaphoreType.DMA
        hbm = pl.BlockSpec(memory_space=pl.ANY)
        return pl.pallas_call(
            moe_kernel,
            out_shape=jax.ShapeDtypeStruct((tok, dim), bf16),
            in_specs=[hbm] * 7,
            out_specs=hbm,
            scratch_shapes=[
                pltpu.VMEM((PAIR_SLOTS, 2, dim, inner), bf16),
                pltpu.VMEM((4, tok, dim), bf16),
                pltpu.VMEM((4, top_k, tok), jnp.int32),
                pltpu.VMEM((dim // LANES, LANES), bf16),
                pltpu.VMEM((n_exp, dim), bf16),
                pltpu.VMEM((tok, dim), bf16),
                pltpu.VMEM((n_exp, tok), f32),
                pltpu.VMEM((local_exp, 4 * cap, dim), bf16),
                pltpu.VMEM((local_exp, 4 * cap, inner), bf16),
                pltpu.VMEM((4, 3 * tok, local_exp * cap), bf16),
                pltpu.VMEM((4, local_exp * cap, BLOCK), bf16),
                pltpu.VMEM((nb, 4, tok, BLOCK), f32),
                pltpu.VMEM((nb, 2, tok, BLOCK), f32),
                pltpu.VMEM((nb, tok, BLOCK), f32),
                pltpu.VMEM((nb, tok, BLOCK), f32),
                pltpu.VMEM((nb, tok, BLOCK), f32),
                pltpu.VMEM((nb, tok, BLOCK), f32),
                pltpu.VMEM((tok, dim), bf16),
                dma((PAIR_SLOTS, 4)),
                dma((4,)),
                dma((3,)), dma((3,)), dma((3,)), dma((3,)),
                dma((nb, 2)), dma((nb, 2)),
                dma((nb,)), dma((nb,)), dma((nb,)), dma((nb,)), dma((nb,)),
            ],
            compiler_params=pltpu.CompilerParams(
                collective_id=0, has_side_effects=True, vmem_limit_bytes=67043328,
            ),
            name="moe",
        )(
            hidden, expert_ids.T, norm_w.reshape(dim // LANES, LANES), router_w.T,
            w_gate, w_up, w_down.reshape(local_exp * inner, dim),
        )

    token_spec = P(("dp", "ep"), None)
    return jax.shard_map(
        per_device, mesh=mesh,
        in_specs=(token_spec, token_spec, P(None), P(None, None), P("ep", None, "tp"), P("ep", None, "tp"), P("ep", "tp", None)),
        out_specs=token_spec, check_vma=False,
    )
```

time: 310 us -> 64.5 us (0.21)
  waiting for transfers between devices: 145 us -> 0 us
  Pallas kernels: 0 us -> 62.7 us
  blocking collectives: 52.5 us -> 0 us
  matrix products: 43 us -> 0 us
  local copies, waits for them, and re-layouts: 39.2 us -> 1.67 us
  between operations: 13.6 us -> 0.01 us
  other arithmetic: 10.3 us -> 0 us
  starting transfers between devices: 5.17 us -> 0 us
    psum x1 -> x0, waiting for transfers between devices: 102 us -> none  [per_device(): expert_out = lax.psum(part_out, 'tp')]
    pallas_call x0 -> x1, Pallas kernels: none -> 62.7 us  [per_device(): pl.pallas_call(moe_kernel, out_shape=jax.ShapeDtypeStruct((tok, dim), bf1...]
    all_to_all x1 -> x0, blocking collectives: 52.5 us -> none  [per_device(): lax.all_to_all(send_rows, 'ep', 0, 2, tiled=True)]
    all_to_all x1 -> x0, waiting for transfers between devices: 43 us -> none  [per_device(): lax.all_to_all(expert_out.reshape(1, local_exp, ep_size * row_limit, mode...]
    dot_general x3 -> x0, matrix products: 43 us -> none  [the longest x1 28.2 us: per_device(): jnp.einsum('erf,efd->erd', act_rows, w_down, preferred_element_type=jnp.f...]
    gather x7 -> x0, local copies, waits for them, and re-layouts: 17.4 us -> none  [the longest x1 7.18 us: per_device(): back_rows.reshape(n_slots, model_dim)[slot_dest]]
    all_to_all x2 -> x0, local copies, waits for them, and re-layouts: 8.94 us -> none  [the longest x1 6.51 us: per_device(): lax.all_to_all(expert_out.reshape(1, local_exp, ep_size * row_limit, mode...]
    psum x1 -> x0, local copies, waits for them, and re-layouts: 6.45 us -> none  [per_device(): expert_out = lax.psum(part_out, 'tp')]
  transfers between devices with their start and end apart: 2 -> 0, of which waited for: 2 -> 0; matrix products, arithmetic and copies ran while one was open for 1% -> 0% of each run, Pallas kernels for 0% -> 0%
where the time goes in v1:
time: 64.5 us; the launch traced here: 64.4 us
  Pallas kernels  62.7 us (97%)
  local copies, waits for them, and re-layouts  1.67 us (3%)
    pallas_call x1, Pallas kernels, per_device(): pl.pallas_call(moe_kernel, out_shape=jax.ShapeDtypeStruct((tok, dim), bf1...  62.7 us
    unnamed x1, local copies, waits for them, and re-layouts  1.67 us

profile of v1, /device:TPU:0, one launch (start us, length us, event | category | flops | bytes accessed | tf_op | source)
XLA Modules:
  0.0 64.4 jit_solution(3898333326960811795)
XLA Ops:
  0.0 62.7 %moe.1 = bf16[64,2048]{1,0:T(8,128)(2,1)} custom-call(bf16[64,2048]{1,0:T(8,128)(2,1)} %hid_hbm.1, s32[8,64]{1,0:T(8,128)} %bitcast.6, bf16[16,128]{1,0:T(8,128)(2,1)} %bitcast.7, bf16[64,2048]{1,0:T(8,128)(2,1)} %bitcast.5, bf16[16,2048,512]{2,1,0:T(8,128)(2,1)} %gate_hbm.1, bf16[16,2048,512]{2,1,0:T(8,128)(2,1)} %up_hbm.1, bf16[8192,2048]{1,0:T(8,128)(2,1)} %bitcast.4), custom_call_target="tpu_custom_call" | custom-call | tf_op jit(solution)/shard_map/moe/pallas_call | solution.py:272
  62.7 1.7 %copy.9 = bf16[64,2048]{1,0:T(8,128)(2,1)} copy(bf16[64,2048]{1,0:T(8,128)(2,1)} %moe.1) | data formatting | bytes 524288

commit v2 on v1

--- a/solution.py
+++ b/solution.py
@@ -8,22 +8,67 @@
 NORM_EPS = 1e-6
 LANES = 128
 BLOCK = 256
-PAIR_SLOTS = 10
+PAIR_SLOTS = 11
+BLOCKS = (
+    (0, 0, 256, "XR"), (1, 0, 256, "YR"), (2, 0, 256, "YR"), (3, 0, 256, "XR"), (4, 0, 256, "YR"),
+    (5, 0, 256, "XR"), (6, 0, 256, "YR"), (7, 0, 256, "X"),
+)
+STAGES = {"X": 3, "XR": 4, "YR": 4, "D": 2}
+LINK, HOP, SIB, MATMULS, ADDS, PIECE, LEAD = 1.52, 2.05, 0.95, 0.78, 0.12, 1.22, 2.0
+
+
+def static_order():
+    x_free = y_free = now = 0.0
+    ready, order = {}, []
+
+    def run(b, stage):
+        nonlocal x_free, y_free, now
+        mode, units = BLOCKS[b][3], LINK * BLOCKS[b][2] / BLOCK
+        now = max(now, ready.pop((b, stage))) + ADDS
+        order.append(("stage", b, stage))
+        if stage + 1 >= STAGES[mode]:
+            return
+        if mode == "D":
+            x_free = max(x_free, now) + 2 * units
+            y_free = max(y_free, now) + 2 * units
+            then = max(x_free, y_free) + HOP + 0.8
+        elif stage < 2 and (stage == 0) == (mode != "YR"):
+            then = x_free = max(x_free, now) + (units / 2 if mode == "YR" else units)
+            then += HOP
+        else:
+            share = 0.25 if stage == 2 else 0.5 if mode == "XR" else 1.0
+            then = y_free = max(y_free, now) + units * share
+            then += HOP
+        ready[(b, stage + 1)] = then
+
+    for b, (piece, first, width, _) in enumerate(BLOCKS):
+        arrive = PIECE * (piece + (first + width) / BLOCK) - LEAD
+        while ready:
+            key = min(ready, key=ready.get)
+            if ready[key] > now and ready[key] + ADDS > arrive:
+                break
+            run(*key)
+        now = max(now, arrive) + MATMULS
+        order.append(("block", b, 0))
+        ready[(b, 0)] = now + SIB
+    while ready:
+        run(*min(ready, key=ready.get))
+    return order
 
 
 def moe_kernel(
-    hid_hbm, ids_hbm, norm_hbm, router_hbm, gate_hbm, up_hbm, down_hbm, out_hbm,
+    hid_hbm, ids_hbm, norm_hbm, router_hbm, gate_hbm, up_hbm, down_hbm, out,
     w_buf, hid, ids, norm_buf, router, normed, prob_buf, x_buf, act, g3, y_buf,
-    part, sib_in, x_out, x_in, y_out, y_in, out_buf,
+    part, sib_in, x_out, x_in, y_out, y_in, z_in, fin, fin_in,
     w_sem, load_sem, hid_send, hid_recv, ids_send, ids_recv,
-    sib_send, sib_recv, xs_sem, xr_sem, ys_sem, yr_sem, out_sem,
+    sib_send, sib_recv, xs_sem, xr_sem, ys_sem, yr_sem, zs_sem, zr_sem, fs_sem, fr_sem,
 ):
     me = lax.axis_index("ep")
     tp = lax.axis_index("tp")
     sib = me + 1 - 2 * (me % 2)
     across = (me + 2) % 4
     twin = 1 - tp
-    sib_id, across_id, twin_id = {"ep": sib}, {"ep": across}, {"tp": twin}
+    sib_id, across_id, twin_id, diag_id = {"ep": sib}, {"ep": across}, {"tp": twin}, {"ep": across, "tp": twin}
 
     tok, dim = hid.shape[1], hid.shape[2]
     n_exp = router.shape[0]
@@ -31,7 +76,7 @@
     inner = act.shape[2]
     top_k = ids.shape[1]
     cap = x_buf.shape[1] // 4
-    n_blocks = dim // BLOCK
+    n_pieces = dim // BLOCK
     f32, bf16 = jnp.float32, jnp.bfloat16
 
     def gate_copies(pair):
@@ -41,34 +86,24 @@
             pltpu.make_async_copy(up_hbm.at[pair], w_buf.at[slot, 1], w_sem.at[slot, 1]),
         ]
 
-    def down_copy(block, quad):
-        slot = (local_exp + block) % PAIR_SLOTS
+    def down_copy(piece, quad, first, width):
+        slot = (local_exp + piece) % PAIR_SLOTS
         rows = 4 * inner
         return pltpu.make_async_copy(
-            down_hbm.at[pl.ds(quad * rows, rows), pl.ds(block * BLOCK, BLOCK)],
-            w_buf.at[slot, quad // 2, :, pl.ds((quad % 2) * BLOCK, BLOCK)],
-            w_sem.at[slot, quad],
+            down_hbm.at[pl.ds(quad * rows, rows), pl.ds(piece * BLOCK + first, width)],
+            w_buf.at[slot, quad // 2, :, pl.ds((quad % 2) * BLOCK + first, width)],
+            w_sem.at[slot, quad + 4 * (first // LANES)],
         )
 
     def start_pair(pair):
-        if isinstance(pair, int):
-            if pair < local_exp:
-                for c in gate_copies(pair):
-                    c.start()
-            elif pair < local_exp + n_blocks:
-                for q in range(4):
-                    down_copy(pair - local_exp, q).start()
-            return
-
-        @pl.when(pair < local_exp)
-        def _():
+        if pair < local_exp:
             for c in gate_copies(pair):
-                c.start()
-
-        @pl.when((pair >= local_exp) & (pair < local_exp + n_blocks))
-        def _():
-            for q in range(4):
-                down_copy(pair - local_exp, q).start()
+                c.start(priority=1)
+        elif pair < local_exp + n_pieces:
+            for piece, first, width, _ in BLOCKS:
+                if piece == pair - local_exp:
+                    for q in range(4):
+                        down_copy(piece, q, first, width).start(priority=1)
 
     hid_load = pltpu.make_async_copy(hid_hbm, hid.at[0], load_sem.at[0])
     ids_load = pltpu.make_async_copy(ids_hbm, ids.at[0], load_sem.at[1])
@@ -80,9 +115,9 @@
         start_pair(pair)
 
     barrier = pltpu.get_barrier_semaphore()
-    for dev in (sib_id, across_id, twin_id):
+    for dev in (sib_id, across_id, twin_id, diag_id):
         pl.semaphore_signal(barrier, inc=1, device_id=dev, device_id_type=pl.DeviceIdType.MESH)
-    pl.semaphore_wait(barrier, 3)
+    pl.semaphore_wait(barrier, 4)
 
     def remote(src, dst, ssem, rsem, dev):
         return pltpu.make_async_remote_copy(
@@ -162,100 +197,159 @@
         c.wait_recv()
     prepare(3)
 
-    def expert_step(e, carry):
-        slot = e % PAIR_SLOTS
-        gate_copy, up_copy = gate_copies(e)
-        gate_copy.wait()
-        gate_pre = jnp.dot(x_buf[e], w_buf[slot, 0], preferred_element_type=f32)
-        up_copy.wait()
-        up_pre = jnp.dot(x_buf[e], w_buf[slot, 1], preferred_element_type=f32)
-        act[e] = (jax.nn.silu(gate_pre) * up_pre).astype(bf16)
-
+    def twice(rows):
+        return jnp.concatenate([rows, rows], axis=0)
+
+    def experts(first, count):
+        for i in range(count):
+            for c in gate_copies(first + i):
+                c.wait()
+        for i in range(count):
+            e = first + i
+            slot = e % PAIR_SLOTS
+            x = twice(x_buf[e])
+            gate_pre = jnp.dot(x, w_buf[slot, 0], preferred_element_type=f32)[: 4 * cap]
+            up_pre = jnp.dot(x, w_buf[slot, 1], preferred_element_type=f32)[: 4 * cap]
+            act[e] = (jax.nn.silu(gate_pre) * up_pre).astype(bf16)
+
+    more_pairs = local_exp - PAIR_SLOTS
+
+    def expert_step(i, carry):
+        experts(i, 1)
+        for c in gate_copies(i + PAIR_SLOTS):
+            c.start(priority=1)
+        return carry
+
+    lax.fori_loop(0, more_pairs, expert_step, 0)
+    for e in range(more_pairs, local_exp):
+        experts(e, 1)
         start_pair(e + PAIR_SLOTS)
-        return carry
-
-    lax.fori_loop(0, local_exp, expert_step, 0)
+
+    def cols_of(b):
+        piece, first, width, _ = BLOCKS[b]
+        return piece * BLOCK + first, width
 
     def sib_copies(b):
+        w = pl.ds(0, BLOCKS[b][2])
         return [
-            remote(part.at[b, src], sib_in.at[b, i], sib_send.at[b, i], sib_recv.at[b, i], sib_id)
+            remote(part.at[b, src, :, w], sib_in.at[b, i, :, w], sib_send.at[b, i], sib_recv.at[b, i], sib_id)
             for i, src in ((1, 3), (0, 1))
         ]
 
+    def lanes(b, which):
+        w = BLOCKS[b][2]
+        if which == "all":
+            return pl.ds(0, w)
+        return pl.ds(pl.multiple_of((tp if which == "mine" else twin) * (w // 2), LANES), w // 2)
+
     def x_copy(b):
-        return remote(x_out.at[b], x_in.at[b], xs_sem.at[b], xr_sem.at[b], across_id)
+        w = lanes(b, "mine" if BLOCKS[b][3] == "YR" else "all")
+        return remote(x_out.at[b, :, w], x_in.at[b, :, w], xs_sem.at[b], xr_sem.at[b], across_id)
 
     def y_copy(b):
-        return remote(y_out.at[b], y_in.at[b], ys_sem.at[b], yr_sem.at[b], twin_id)
-
-    def out_copy(b):
-        cols = pl.ds(b * BLOCK, BLOCK)
-        return pltpu.make_async_copy(out_buf.at[:, cols], out_hbm.at[:, cols], out_sem.at[b])
-
-    def down_quad(b, q):
-        slot = (local_exp + b) % PAIR_SLOTS
-        down_copy(b, q).wait()
-        for i in range(4):
-            e = 4 * q + i
-            w = w_buf[slot, q // 2, pl.ds(i * inner, inner), pl.ds((q % 2) * BLOCK, BLOCK)]
-            y = jnp.dot(act[e], w, preferred_element_type=f32).astype(bf16)
-            for k in range(4):
-                y_buf[k, pl.ds(e * cap, cap), :] = y[k * cap : (k + 1) * cap, :]
-
-    def combine(b):
+        w = lanes(b, "theirs" if BLOCKS[b][3] in ("XR", "YR") else "all")
+        return remote(y_out.at[b, :, w], y_in.at[b, :, w], ys_sem.at[b], yr_sem.at[b], twin_id)
+
+    def z_copy(b):
+        yr = BLOCKS[b][3] == "YR"
+        w = lanes(b, "theirs" if yr else "all")
+        return remote(x_out.at[b, :, w], z_in.at[b, :, w], zs_sem.at[b], zr_sem.at[b], twin_id if yr else diag_id)
+
+    def fin_copy(b):
+        return remote(fin.at[b], fin_in.at[b], fs_sem.at[b], fr_sem.at[b], twin_id)
+
+    def compute(b):
+        piece, first, width, _ = BLOCKS[b]
+        slot = (local_exp + piece) % PAIR_SLOTS
+        for q in range(4):
+            down_copy(piece, q, first, width).wait()
+        for q in range(4):
+            for i in range(4):
+                e = 4 * q + i
+                w = w_buf[slot, q // 2, pl.ds(i * inner, inner), pl.ds((q % 2) * BLOCK + first, width)]
+                y = jnp.dot(twice(act[e]), w, preferred_element_type=f32)[: 4 * cap].astype(bf16)
+                for k in range(4):
+                    y_buf[k, pl.ds(e * cap, cap), pl.ds(0, width)] = y[k * cap : (k + 1) * cap, :]
         for k in (3, 1, 2, 0):
-            s = jnp.dot(g3[k], y_buf[k], preferred_element_type=f32)
-            part[b, k] = s[:tok] + s[tok : 2 * tok] + s[2 * tok :]
+            s = jnp.dot(g3[k], y_buf[k, :, pl.ds(0, width)], preferred_element_type=f32)
+            part[b, k, :, pl.ds(0, width)] = s[:tok] + s[tok : 2 * tok] + s[2 * tok :]
             if k == 1:
                 for c in sib_copies(b):
                     c.start()
 
-    def stage_x(b):
-        first, second = sib_copies(b)
-        first.wait_recv()
-        x_out[b] = part[b, 2] + sib_in[b, 1]
-        x_copy(b).start()
-        second.wait_recv()
-        y_out[b] = part[b, 0] + sib_in[b, 0]
-
-    def stage_y(b):
-        x_copy(b).wait_recv()
-        y_out[b] = y_out[b] + x_in[b]
-        y_copy(b).start()
-
-    def finish(b):
-        y_copy(b).wait_recv()
-        cols = pl.ds(b * BLOCK, BLOCK)
-        out_buf[:, cols] = (hid[0, :, cols].astype(f32) + (y_out[b] + y_in[b])).astype(bf16)
-        out_copy(b).start()
-
-    Y_LAG, OUT_LAG = 4, 7
-    for b in range(n_blocks):
-        for q in range(4):
-            down_quad(b, q)
-            if q == 2 and b >= 1:
-                stage_x(b - 1)
-        combine(b)
-        start_pair(local_exp + b + PAIR_SLOTS)
-        if b >= Y_LAG:
-            stage_y(b - Y_LAG)
-        if b >= OUT_LAG:
-            finish(b - OUT_LAG)
-    stage_x(n_blocks - 1)
-    for b in range(n_blocks - Y_LAG, n_blocks):
-        stage_y(b)
-    for b in range(n_blocks - OUT_LAG, n_blocks):
-        finish(b)
+    def put(b, which, value):
+        start, width = cols_of(b)
+        if which == "all":
+            cols = pl.ds(start, width)
+        else:
+            half = width // 2
+            cols = pl.ds(pl.multiple_of(start + (tp if which == "mine" else twin) * half, LANES), half)
+        if which == "theirs":
+            out[:, cols] = value
+            return None
+        result = (hid[0, :, cols].astype(f32) + value).astype(bf16)
+        out[:, cols] = result
+        return result
+
+    def stage(b, n):
+        mode = BLOCKS[b][3]
+        full, mine = lanes(b, "all"), lanes(b, "mine") if mode in ("XR", "YR") else None
+        if n == 0:
+            first, second = sib_copies(b)
+            first.wait_recv()
+            x_out[b, :, full] = part[b, 2, :, full] + sib_in[b, 1, :, full]
+            (z_copy if mode == "YR" else x_copy)(b).start()
+            if mode == "D":
+                z_copy(b).start()
+            second.wait_recv()
+            y_out[b, :, full] = part[b, 0, :, full] + sib_in[b, 0, :, full]
+            if mode in ("YR", "D"):
+                y_copy(b).start()
+        elif mode == "D":
+            x_copy(b).wait_recv()
+            y_copy(b).wait_recv()
+            z_copy(b).wait_recv()
+            put(b, "all", (y_out[b, :, full] + x_in[b, :, full]) + (y_in[b, :, full] + z_in[b, :, full]))
+        elif n == 1 and mode == "YR":
+            z_copy(b).wait_recv()
+            x_out[b, :, mine] = x_out[b, :, mine] + z_in[b, :, mine]
+            x_copy(b).start()
+            y_copy(b).wait_recv()
+            y_out[b, :, mine] = y_out[b, :, mine] + y_in[b, :, mine]
+        elif n == 1:
+            x_copy(b).wait_recv()
+            y_out[b, :, full] = y_out[b, :, full] + x_in[b, :, full]
+            y_copy(b).start()
+        elif mode == "X":
+            y_copy(b).wait_recv()
+            put(b, "all", y_out[b, :, full] + y_in[b, :, full])
+        elif n == 2:
+            (x_copy if mode == "YR" else y_copy)(b).wait_recv()
+            other = x_in if mode == "YR" else y_in
+            fin[b] = put(b, "mine", y_out[b, :, mine] + other[b, :, mine])
+            fin_copy(b).start()
+        else:
+            fin_copy(b).wait_recv()
+            put(b, "theirs", fin_in[b])
+
+    for kind, b, n in static_order():
+        if kind == "block":
+            compute(b)
+        else:
+            stage(b, n)
 
     for j in range(3):
         for c in row_copies(j):
             c.wait_send()
-    for b in range(n_blocks):
+    for b, (_, _, _, mode) in enumerate(BLOCKS):
         for c in sib_copies(b):
             c.wait_send()
         x_copy(b).wait_send()
         y_copy(b).wait_send()
-        out_copy(b).wait()
+        if mode in ("YR", "D"):
+            z_copy(b).wait_send()
+        if mode in ("YR", "XR"):
+            fin_copy(b).wait_send()
 
 
 def solution(mesh):
@@ -265,15 +359,15 @@
         n_exp = router_w.shape[1]
         local_exp, _, inner = w_gate.shape
         cap = 8 * ((2 * top_k * tok + 8 * n_exp - 1) // (8 * n_exp))
-        nb = dim // BLOCK
+        nb = len(BLOCKS)
         f32, bf16 = jnp.float32, jnp.bfloat16
         dma = pltpu.SemaphoreType.DMA
         hbm = pl.BlockSpec(memory_space=pl.ANY)
         return pl.pallas_call(
             moe_kernel,
-            out_shape=jax.ShapeDtypeStruct((tok, dim), bf16),
+            out_shape=pltpu.VMEM((tok, dim), bf16),
             in_specs=[hbm] * 7,
-            out_specs=hbm,
+            out_specs=pl.BlockSpec(memory_space=pltpu.VMEM),
             scratch_shapes=[
                 pltpu.VMEM((PAIR_SLOTS, 2, dim, inner), bf16),
                 pltpu.VMEM((4, tok, dim), bf16),
@@ -292,15 +386,17 @@
                 pltpu.VMEM((nb, tok, BLOCK), f32),
                 pltpu.VMEM((nb, tok, BLOCK), f32),
                 pltpu.VMEM((nb, tok, BLOCK), f32),
-                pltpu.VMEM((tok, dim), bf16),
-                dma((PAIR_SLOTS, 4)),
+                pltpu.VMEM((nb, tok, BLOCK), f32),
+                pltpu.VMEM((nb, tok, LANES), bf16),
+                pltpu.VMEM((nb, tok, LANES), bf16),
+                dma((PAIR_SLOTS, 8)),
                 dma((4,)),
                 dma((3,)), dma((3,)), dma((3,)), dma((3,)),
                 dma((nb, 2)), dma((nb, 2)),
-                dma((nb,)), dma((nb,)), dma((nb,)), dma((nb,)), dma((nb,)),
+                *[dma((nb,))] * 8,
             ],
             compiler_params=pltpu.CompilerParams(
-                collective_id=0, has_side_effects=True, vmem_limit_bytes=67043328,
+                collective_id=0, has_side_effects=True, vmem_limit_bytes=62 * 2**20,
             ),
             name="moe",
         )(

time: 64.5 us -> 46.2 us (0.72)
  Pallas kernels: 62.7 us -> 45.4 us
  local copies, waits for them, and re-layouts: 1.67 us -> 0.71 us
    pallas_call x1, Pallas kernels: 62.7 us -> 45.4 us  [per_device(): pl.pallas_call(moe_kernel, out_shape=pltpu.VMEM((tok, dim), bf16), in_spe...]
    unnamed x1, local copies, waits for them, and re-layouts: 1.67 us -> 0.71 us
where the time goes in v2:
time: 46.2 us; the launch traced here: 46.1 us
  Pallas kernels  45.4 us (98%)
  local copies, waits for them, and re-layouts  0.71 us (2%)
    pallas_call x1, Pallas kernels, per_device(): pl.pallas_call(moe_kernel, out_shape=pltpu.VMEM((tok, dim), bf16), in_spe...  45.4 us

profile of v2, /device:TPU:0, one launch (start us, length us, event | category | flops | bytes accessed | tf_op | source)
XLA Modules:
  0.0 46.1 jit_solution(17762193460627859739)
XLA Ops:
  0.0 45.4 %moe.1 = bf16[64,2048]{1,0:T(8,128)(2,1)S(1)} custom-call(bf16[64,2048]{1,0:T(8,128)(2,1)} %hid_hbm.1, s32[8,64]{1,0:T(8,128)} %bitcast.6, bf16[16,128]{1,0:T(8,128)(2,1)} %bitcast.7, bf16[64,2048]{1,0:T(8,128)(2,1)} %bitcast.5, bf16[16,2048,512]{2,1,0:T(8,128)(2,1)} %gate_hbm.1, bf16[16,2048,512]{2,1,0:T(8,128)(2,1)} %up_hbm.1, bf16[8192,2048]{1,0:T(8,128)(2,1)} %bitcast.4), custom_call_target="tpu_custom_call" | custom-call | tf_op jit(solution)/shard_map/moe/pallas_call | solution.py:366
  45.4 0.7 %copy.9 = bf16[64,2048]{1,0:T(8,128)(2,1)} copy(bf16[64,2048]{1,0:T(8,128)(2,1)S(1)} %moe.1) | data formatting | bytes 524288

commit v3 on v2

--- a/solution.py
+++ b/solution.py
@@ -10,11 +10,11 @@
 BLOCK = 256
 PAIR_SLOTS = 11
 BLOCKS = (
-    (0, 0, 256, "XR"), (1, 0, 256, "YR"), (2, 0, 256, "YR"), (3, 0, 256, "XR"), (4, 0, 256, "YR"),
-    (5, 0, 256, "XR"), (6, 0, 256, "YR"), (7, 0, 256, "X"),
+    (0, 0, 256, "X"), (1, 0, 256, "YR"), (2, 0, 256, "YR"), (3, 0, 256, "XR"), (4, 0, 256, "YR"),
+    (5, 0, 256, "X"), (6, 0, 256, "YR"), (7, 0, 256, "X"),
 )
-STAGES = {"X": 3, "XR": 4, "YR": 4, "D": 2}
-LINK, HOP, SIB, MATMULS, ADDS, PIECE, LEAD = 1.52, 2.05, 0.95, 0.78, 0.12, 1.22, 2.0
+STAGES = {"X": 3, "XR": 4, "YR": 4}
+LINK, HOP, SIB, MATMULS, ADDS, PIECE, LEAD = 1.52, 2.05, 0.95, 0.78, 0.12, 1.22, 0.8
 
 
 def static_order():
@@ -28,11 +28,7 @@
         order.append(("stage", b, stage))
         if stage + 1 >= STAGES[mode]:
             return
-        if mode == "D":
-            x_free = max(x_free, now) + 2 * units
-            y_free = max(y_free, now) + 2 * units
-            then = max(x_free, y_free) + HOP + 0.8
-        elif stage < 2 and (stage == 0) == (mode != "YR"):
+        if stage < 2 and (stage == 0) == (mode != "YR"):
             then = x_free = max(x_free, now) + (units / 2 if mode == "YR" else units)
             then += HOP
         else:
@@ -68,7 +64,7 @@
     sib = me + 1 - 2 * (me % 2)
     across = (me + 2) % 4
     twin = 1 - tp
-    sib_id, across_id, twin_id, diag_id = {"ep": sib}, {"ep": across}, {"tp": twin}, {"ep": across, "tp": twin}
+    sib_id, across_id, twin_id = {"ep": sib}, {"ep": across}, {"tp": twin}
 
     tok, dim = hid.shape[1], hid.shape[2]
     n_exp = router.shape[0]
@@ -115,9 +111,9 @@
         start_pair(pair)
 
     barrier = pltpu.get_barrier_semaphore()
-    for dev in (sib_id, across_id, twin_id, diag_id):
+    for dev in (sib_id, across_id, twin_id):
         pl.semaphore_signal(barrier, inc=1, device_id=dev, device_id_type=pl.DeviceIdType.MESH)
-    pl.semaphore_wait(barrier, 4)
+    pl.semaphore_wait(barrier, 3)
 
     def remote(src, dst, ssem, rsem, dev):
         return pltpu.make_async_remote_copy(
@@ -212,18 +208,23 @@
             up_pre = jnp.dot(x, w_buf[slot, 1], preferred_element_type=f32)[: 4 * cap]
             act[e] = (jax.nn.silu(gate_pre) * up_pre).astype(bf16)
 
-    more_pairs = local_exp - PAIR_SLOTS
+    more_pairs = (local_exp - PAIR_SLOTS) // 2
 
     def expert_step(i, carry):
-        experts(i, 1)
-        for c in gate_copies(i + PAIR_SLOTS):
-            c.start(priority=1)
+        experts(2 * i, 2)
+        for j in range(2):
+            for c in gate_copies(2 * i + j + PAIR_SLOTS):
+                c.start(priority=1)
         return carry
 
     lax.fori_loop(0, more_pairs, expert_step, 0)
-    for e in range(more_pairs, local_exp):
-        experts(e, 1)
-        start_pair(e + PAIR_SLOTS)
+    e = 2 * more_pairs
+    while e < local_exp:
+        count = 2 if e < local_exp - 2 else 1
+        experts(e, count)
+        for j in range(count):
+            start_pair(e + j + PAIR_SLOTS)
+        e += count
 
     def cols_of(b):
         piece, first, width, _ = BLOCKS[b]
@@ -251,9 +252,8 @@
         return remote(y_out.at[b, :, w], y_in.at[b, :, w], ys_sem.at[b], yr_sem.at[b], twin_id)
 
     def z_copy(b):
-        yr = BLOCKS[b][3] == "YR"
-        w = lanes(b, "theirs" if yr else "all")
-        return remote(x_out.at[b, :, w], z_in.at[b, :, w], zs_sem.at[b], zr_sem.at[b], twin_id if yr else diag_id)
+        w = lanes(b, "theirs")
+        return remote(x_out.at[b, :, w], z_in.at[b, :, w], zs_sem.at[b], zr_sem.at[b], twin_id)
 
     def fin_copy(b):
         return remote(fin.at[b], fin_in.at[b], fs_sem.at[b], fr_sem.at[b], twin_id)
@@ -299,17 +299,10 @@
             first.wait_recv()
             x_out[b, :, full] = part[b, 2, :, full] + sib_in[b, 1, :, full]
             (z_copy if mode == "YR" else x_copy)(b).start()
-            if mode == "D":
-                z_copy(b).start()
             second.wait_recv()
             y_out[b, :, full] = part[b, 0, :, full] + sib_in[b, 0, :, full]
-            if mode in ("YR", "D"):
+            if mode == "YR":
                 y_copy(b).start()
-        elif mode == "D":
-            x_copy(b).wait_recv()
-            y_copy(b).wait_recv()
-            z_copy(b).wait_recv()
-            put(b, "all", (y_out[b, :, full] + x_in[b, :, full]) + (y_in[b, :, full] + z_in[b, :, full]))
         elif n == 1 and mode == "YR":
             z_copy(b).wait_recv()
             x_out[b, :, mine] = x_out[b, :, mine] + z_in[b, :, mine]
@@ -346,7 +339,7 @@
             c.wait_send()
         x_copy(b).wait_send()
         y_copy(b).wait_send()
-        if mode in ("YR", "D"):
+        if mode == "YR":
             z_copy(b).wait_send()
         if mode in ("YR", "XR"):
             fin_copy(b).wait_send()

time: 46.2 us -> 45.6 us (0.987)
  Pallas kernels: 45.4 us -> 44.8 us
    pallas_call x1, Pallas kernels: 45.4 us -> 44.8 us  [per_device(): pl.pallas_call(moe_kernel, out_shape=pltpu.VMEM((tok, dim), bf16), in_spe...]
where the time goes in v3:
time: 45.6 us; the launch traced here: 45.5 us
  Pallas kernels  44.8 us (98%)
  local copies, waits for them, and re-layouts  0.71 us (2%)
    pallas_call x1, Pallas kernels, per_device(): pl.pallas_call(moe_kernel, out_shape=pltpu.VMEM((tok, dim), bf16), in_spe...  44.8 us

profile of v3, /device:TPU:0, one launch (start us, length us, event | category | flops | bytes accessed | tf_op | source)
XLA Modules:
  0.0 45.5 jit_solution(5440067810941536305)
XLA Ops:
  0.0 44.8 %moe.1 = bf16[64,2048]{1,0:T(8,128)(2,1)S(1)} custom-call(bf16[64,2048]{1,0:T(8,128)(2,1)} %hid_hbm.1, s32[8,64]{1,0:T(8,128)} %bitcast.6, bf16[16,128]{1,0:T(8,128)(2,1)} %bitcast.7, bf16[64,2048]{1,0:T(8,128)(2,1)} %bitcast.5, bf16[16,2048,512]{2,1,0:T(8,128)(2,1)} %gate_hbm.1, bf16[16,2048,512]{2,1,0:T(8,128)(2,1)} %up_hbm.1, bf16[8192,2048]{1,0:T(8,128)(2,1)} %bitcast.4), custom_call_target="tpu_custom_call" | custom-call | tf_op jit(solution)/shard_map/moe/pallas_call | solution.py:359
  44.8 0.7 %copy.9 = bf16[64,2048]{1,0:T(8,128)(2,1)} copy(bf16[64,2048]{1,0:T(8,128)(2,1)S(1)} %moe.1) | data formatting | bytes 524288

commit v4 on v3

--- a/solution.py
+++ b/solution.py
@@ -10,11 +10,11 @@
 BLOCK = 256
 PAIR_SLOTS = 11
 BLOCKS = (
-    (0, 0, 256, "X"), (1, 0, 256, "YR"), (2, 0, 256, "YR"), (3, 0, 256, "XR"), (4, 0, 256, "YR"),
-    (5, 0, 256, "X"), (6, 0, 256, "YR"), (7, 0, 256, "X"),
+    (0, 0, 256, "X"), (1, 0, 256, "XR"), (2, 0, 256, "YR"), (3, 0, 256, "XR"), (4, 0, 256, "X"),
+    (5, 0, 256, "YR"), (6, 0, 256, "X"), (7, 0, 256, "X"),
 )
 STAGES = {"X": 3, "XR": 4, "YR": 4}
-LINK, HOP, SIB, MATMULS, ADDS, PIECE, LEAD = 1.52, 2.05, 0.95, 0.78, 0.12, 1.22, 0.8
+LINK, HOP, SIB, MATMULS, ADDS, PIECE, LEAD = 1.52, 2.05, 0.95, 0.9, 0.12, 1.3, 0.0
 
 
 def static_order():

time: 45.6 us -> 45.7 us (level)
  no operation moved by 1% of the time
where the time goes in v4:
time: 45.7 us; the launch traced here: 45.6 us
  Pallas kernels  44.9 us (98%)
  local copies, waits for them, and re-layouts  0.71 us (2%)
    pallas_call x1, Pallas kernels, per_device(): pl.pallas_call(moe_kernel, out_shape=pltpu.VMEM((tok, dim), bf16), in_spe...  44.9 us

profile of v4, /device:TPU:0, one launch (start us, length us, event | category | flops | bytes accessed | tf_op | source)
XLA Modules:
  0.0 45.6 jit_solution(5089608333824026339)
XLA Ops:
  0.0 44.9 %moe.1 = bf16[64,2048]{1,0:T(8,128)(2,1)S(1)} custom-call(bf16[64,2048]{1,0:T(8,128)(2,1)} %hid_hbm.1, s32[8,64]{1,0:T(8,128)} %bitcast.6, bf16[16,128]{1,0:T(8,128)(2,1)} %bitcast.7, bf16[64,2048]{1,0:T(8,128)(2,1)} %bitcast.5, bf16[16,2048,512]{2,1,0:T(8,128)(2,1)} %gate_hbm.1, bf16[16,2048,512]{2,1,0:T(8,128)(2,1)} %up_hbm.1, bf16[8192,2048]{1,0:T(8,128)(2,1)} %bitcast.4), custom_call_target="tpu_custom_call" | custom-call | tf_op jit(solution)/shard_map/moe/pallas_call | solution.py:359
  44.9 0.7 %copy.9 = bf16[64,2048]{1,0:T(8,128)(2,1)} copy(bf16[64,2048]{1,0:T(8,128)(2,1)S(1)} %moe.1) | data formatting | bytes 524288
